TPU v7x, 32 devices: a whole 2x2x4 slice. The times are simulated.
32 devices in a mesh: seq: 8 (over z, x), fsdp: 4 (over y, core).
Axes of the slice: x: 2, y: 2, z: 4, core: 2. Of those that a mesh axis runs over, the one named last changes fastest.
Arguments:
- tokens: bfloat16 [4, 1024, 1536], P('fsdp', 'seq'), may hold values from -6 to 6
- in_weight: bfloat16 [1536, 6400], P('fsdp'), may hold values from -0.15625 to 0.15625
- step_weight: bfloat16 [1536, 48], P('fsdp'), may hold values from -0.15625 to 0.15625
- conv_kernel: bfloat16 [4, 3328], P(None, 'fsdp'), may hold values from -3 to 3
- conv_bias: bfloat16 [3328], P('fsdp'), may hold values from -3 to 3
- step_bias: bfloat16 [48], P('fsdp'), may hold values from -6 to -3
- log_decay: bfloat16 [48], P('fsdp'), may hold values from -7 to 1
- skip_gain: bfloat16 [48], P('fsdp'), may hold values from 0.5 to 1.5
- gate_gain: bfloat16 [3072], P('fsdp'), may hold values from 0.5 to 1.5
- norm_gain: bfloat16 [1536], P('fsdp'), may hold values from 0.5 to 1.5
- out_weight: bfloat16 [3072, 1536], P('fsdp'), may hold values from -0.109375 to 0.109375
- cotangent: bfloat16 [4, 1024, 1536], P('fsdp', 'seq'), may hold values from -6 to 6
Outputs:
- block_out: bfloat16 [4, 1024, 1536], P('fsdp', 'seq')
- input_grad: float32 [4, 1024, 1536], P('fsdp', 'seq')
- in_weight_grad: float32 [1536, 6400], P('fsdp')
- step_weight_grad: float32 [1536, 48], P('fsdp')
- conv_kernel_grad: float32 [4, 3328], P(None, 'fsdp')
- conv_bias_grad: float32 [3328], P('fsdp')
- step_bias_grad: float32 [48], P('fsdp')
- log_decay_grad: float32 [48], P('fsdp')
- skip_gain_grad: float32 [48], P('fsdp')
- gate_gain_grad: float32 [3072], P('fsdp')
- norm_gain_grad: float32 [1536], P('fsdp')
- out_weight_grad: float32 [3072, 1536], P('fsdp')
All inputs are finite; a program needn't handle non-finite values.
Results may differ from a plain program's by a relative error of at most 0.012.
The roundings to bfloat16 on the way count: a program that leaves them out, or rounds other values in their place, can miss the bound.
Values may be sent and summed in bfloat16 or wider, within the bound.
A program may use at most 320 MiB of HBM per device.

v0:
```python
import jax
import jax.numpy as jnp
from jax import lax
from jax.sharding import PartitionSpec as P

N = 128
BLOCK = 256
epsilon = 1e-05
highest = lax.Precision.HIGHEST


def block_step(carried, pieces, decay_rate):
    x_blk, step_blk, b_blk, c_blk = pieces
    cumulative = jnp.cumsum(step_blk * decay_rate[None, :], axis=0).T
    positions = jnp.arange(step_blk.shape[0])
    triangle = positions[:, None] >= positions[None, :]
    log_gap = jnp.where(triangle[None], cumulative[:, :, None] - cumulative[:, None, :], -1e30)
    scores = jnp.dot(c_blk, b_blk.T, precision=highest)
    mixing = jnp.exp(log_gap) * scores[None] * step_blk.T[:, None, :]
    y_inside = jnp.einsum("hij,jhp->ihp", mixing, x_blk, precision=highest)
    y_carried = jnp.exp(cumulative).T[:, :, None] * jnp.einsum(
        "in,hpn->ihp", c_blk, carried, precision=highest
    )
    weighting = jnp.exp(cumulative[:, -1:] - cumulative) * step_blk.T
    renewed = jnp.exp(cumulative[:, -1])[:, None, None] * carried + jnp.einsum(
        "hj,jhp,jn->hpn", weighting, x_blk, b_blk, precision=highest
    )
    return (renewed, y_inside + y_carried)


def ssd_scan(x_heads, step_size, decay_rate, b_conv, c_conv, carried):
    length = step_size.shape[0]
    extent = min(BLOCK, length)
    number = length // extent
    pieces = (
        x_heads.reshape((number, extent) + x_heads.shape[1:]),
        step_size.reshape((number, extent) + step_size.shape[1:]),
        b_conv.reshape(number, extent, -1),
        c_conv.reshape(number, extent, -1),
    )

    def advance(ssm_state, block_in):
        return block_step(ssm_state, block_in, decay_rate)

    finals, outputs = lax.scan(jax.checkpoint(advance), carried, pieces)
    return outputs.reshape(x_heads.shape)


def prepare(extended, raw_steps, conv_kernel, conv_offset, step_bias, log_rates):
    kernel_width = conv_kernel.shape[0]
    length = extended.shape[0] - kernel_width + 1
    summed = conv_offset[None, :] + sum(
        (
            conv_kernel[offset][None, :] * extended[offset : offset + length]
            for offset in range(kernel_width)
        )
    )
    active = jax.nn.silu(summed)
    split_at = active.shape[1] - 2 * N
    step_size = jax.nn.softplus(raw_steps + step_bias[None, :])
    return (
        active[:, :split_at],
        active[:, split_at : split_at + N],
        active[:, split_at + N :],
        step_size,
        -jnp.exp(log_rates),
    )


def mix_out(x_conv, b_conv, c_conv, step_size, decay_rate, gate_in, skip_part, carried):
    length, head_count = step_size.shape
    x_heads = x_conv.reshape(length, head_count, -1)
    result = (
        ssd_scan(x_heads, step_size, decay_rate, b_conv, c_conv, carried)
        + skip_part[None, :, None] * x_heads
    )
    return result.reshape(length, -1) * jax.nn.silu(gate_in)


def rms_forward(values, gains):
    scaling = lax.rsqrt(jnp.mean(values * values, axis=-1, keepdims=True) + epsilon)
    return (values * scaling * gains[None, :], scaling)


def rms_backward(values, gains, scaling, upstream):
    weighted = upstream * gains[None, :]
    gain_grad = jnp.sum(upstream * values * scaling, axis=0)
    inner_mean = jnp.mean(weighted * values, axis=-1, keepdims=True)
    return (scaling * weighted - scaling**3 * values * inner_mean, gain_grad)


def contract(left, right, left_dim, right_dim):
    return lax.dot_general(
        left, right, (((left_dim,), (right_dim,)), ((), ())), preferred_element_type=jnp.float32
    )


def reorder(gradient, axis_pos, outer_count, inner_count):
    moved_axis = jnp.moveaxis(gradient, axis_pos, 0)
    regrouped = moved_axis.reshape((outer_count, inner_count, -1) + moved_axis.shape[1:])
    swapped = jnp.swapaxes(regrouped, 0, 1).reshape(moved_axis.shape)
    return jnp.moveaxis(swapped, 0, axis_pos)


def place_slice(part, total_len, start_at, axis_pos):
    zeros_shape = part.shape[:axis_pos] + (total_len,) + part.shape[axis_pos + 1 :]
    anchor = tuple((start_at if index_pos == axis_pos else 0 for index_pos in range(part.ndim)))
    return lax.dynamic_update_slice(jnp.zeros(zeros_shape, jnp.float32), part, anchor)


def shards(
    tokens,
    in_weight,
    step_weight,
    conv_kernel,
    conv_bias,
    step_bias,
    log_decay,
    skip_gain,
    gate_gain,
    norm_gain,
    out_weight,
    cotangent,
):
    gathered = (
        lax.all_gather(in_weight, "fsdp", axis=0, tiled=True),
        lax.all_gather(step_weight, "fsdp", axis=0, tiled=True),
        lax.all_gather(conv_kernel, "fsdp", axis=1, tiled=True),
        lax.all_gather(conv_bias, "fsdp", axis=0, tiled=True),
        lax.all_gather(step_bias, "fsdp", axis=0, tiled=True),
        lax.all_gather(log_decay, "fsdp", axis=0, tiled=True),
        lax.all_gather(skip_gain, "fsdp", axis=0, tiled=True),
        lax.all_gather(gate_gain, "fsdp", axis=0, tiled=True),
        lax.all_gather(norm_gain, "fsdp", axis=0, tiled=True),
        lax.all_gather(out_weight, "fsdp", axis=0, tiled=True),
    )
    w_in = gathered[0]
    w_step = gathered[1]
    w_out = gathered[9]
    kernel_f = gathered[2].astype(jnp.float32)
    bias_f = gathered[3].astype(jnp.float32)
    step_bias_f = gathered[4].astype(jnp.float32)
    decay_f = gathered[5].astype(jnp.float32)
    skip_f = gathered[6].astype(jnp.float32)
    gate_f = gathered[7].astype(jnp.float32)
    norm_f = gathered[8].astype(jnp.float32)
    inner_width = w_out.shape[0]
    head_count = w_step.shape[1]
    head_size = inner_width // head_count
    kernel_width = kernel_f.shape[0]
    out_cotangent = cotangent[0]
    residual = tokens[0].astype(jnp.float32)
    normed, scale_in = rms_forward(residual, norm_f)
    hidden = normed.astype(jnp.bfloat16)
    projected = jnp.dot(hidden, w_in, preferred_element_type=jnp.float32).astype(jnp.bfloat16)
    raw_steps = jnp.dot(hidden, w_step, preferred_element_type=jnp.float32).astype(jnp.bfloat16)
    seq_count = lax.axis_size("seq")
    position = lax.axis_index("seq")
    head_group = head_count // seq_count
    columns = head_group * head_size
    col_start = position * columns
    head_start = position * head_group
    tiled_bc = jnp.tile(projected[:, 2 * inner_width :], (1, seq_count))
    gate_part, x_part, step_part, bc_part = (
        lax.all_to_all(projected[:, :inner_width], "seq", split_axis=1, concat_axis=0, tiled=True),
        lax.all_to_all(
            projected[:, inner_width : 2 * inner_width],
            "seq",
            split_axis=1,
            concat_axis=0,
            tiled=True,
        ),
        lax.all_to_all(raw_steps, "seq", split_axis=1, concat_axis=0, tiled=True),
        lax.all_to_all(tiled_bc, "seq", split_axis=1, concat_axis=0, tiled=True),
    )
    my_kernel = jnp.concatenate(
        [lax.dynamic_slice_in_dim(kernel_f, col_start, columns, 1), kernel_f[:, inner_width:]],
        axis=1,
    )
    my_bias = jnp.concatenate(
        [lax.dynamic_slice_in_dim(bias_f, col_start, columns, 0), bias_f[inner_width:]], axis=0
    )
    my_step_bias = lax.dynamic_slice_in_dim(step_bias_f, head_start, head_group, 0)
    my_decay = lax.dynamic_slice_in_dim(decay_f, head_start, head_group, 0)
    my_skip = lax.dynamic_slice_in_dim(skip_f, head_start, head_group, 0)
    padding = jnp.zeros((kernel_width - 1, columns + 2 * N), jnp.float32)
    extended = jnp.concatenate(
        [padding, jnp.concatenate([x_part, bc_part], axis=1).astype(jnp.float32)], axis=0
    )
    prepared, pull_prepare = jax.vjp(
        prepare, extended, step_part.astype(jnp.float32), my_kernel, my_bias, my_step_bias, my_decay
    )
    x_conv, b_conv, c_conv, step_size, decay_rate = prepared
    start_state = jnp.zeros((head_group, head_size, N), jnp.float32)
    gated_f, pull_mix = jax.vjp(
        mix_out,
        x_conv,
        b_conv,
        c_conv,
        step_size,
        decay_rate,
        gate_part.astype(jnp.float32),
        my_skip,
        start_state,
    )
    gated_out = lax.all_to_all(
        gated_f.astype(jnp.bfloat16), "seq", split_axis=0, concat_axis=1, tiled=True
    )
    gated_back = gated_out.astype(jnp.float32)
    mixed_f, scale_out = rms_forward(gated_back, gate_f)
    mixed_norm = mixed_f.astype(jnp.bfloat16)
    block_out = (residual + jnp.dot(mixed_norm, w_out, preferred_element_type=jnp.float32)).astype(
        jnp.bfloat16
    )
    out_grad = contract(mixed_norm, out_cotangent, 0, 0)
    mixed_grad = contract(out_cotangent, w_out, 1, 1)
    gated_grad, gate_gain_grad = rms_backward(gated_back, gate_f, scale_out, mixed_grad)
    gated_grad_b = lax.optimization_barrier(gated_grad.astype(jnp.bfloat16))
    gated_grad_h = lax.all_to_all(
        gated_grad_b, "seq", split_axis=1, concat_axis=0, tiled=True
    ).astype(jnp.float32)
    x_grad, b_grad, c_grad, step_grad, rate_grad, gate_in_grad, skip_grad_h, unused = pull_mix(
        gated_grad_h
    )
    ext_grad, raw_grad, kernel_grad_h, bias_grad_h, step_bias_grad_h, decay_grad_h = pull_prepare(
        (x_grad, b_grad, c_grad, step_grad, rate_grad)
    )
    body_grad = ext_grad[kernel_width - 1 :]
    gate_back, x_back, step_back = (
        lax.all_to_all(
            gate_in_grad.astype(jnp.bfloat16), "seq", split_axis=0, concat_axis=1, tiled=True
        ),
        lax.all_to_all(
            body_grad[:, :columns].astype(jnp.bfloat16),
            "seq",
            split_axis=0,
            concat_axis=1,
            tiled=True,
        ),
        lax.all_to_all(
            raw_grad.astype(jnp.bfloat16), "seq", split_axis=0, concat_axis=1, tiled=True
        ),
    )
    bc_back = lax.psum_scatter(
        body_grad[:, columns:].astype(jnp.bfloat16), "seq", scatter_dimension=0, tiled=True
    )
    proj_grad = jnp.concatenate([gate_back, x_back, bc_back], axis=1)
    kernel_grad = jnp.concatenate(
        [
            place_slice(kernel_grad_h[:, :columns], inner_width, col_start, 1),
            kernel_grad_h[:, columns:],
        ],
        axis=1,
    )
    bias_grad = jnp.concatenate(
        [place_slice(bias_grad_h[:columns], inner_width, col_start, 0), bias_grad_h[columns:]],
        axis=0,
    )
    step_bias_grad = place_slice(step_bias_grad_h, head_count, head_start, 0)
    decay_grad = place_slice(decay_grad_h, head_count, head_start, 0)
    skip_grad = place_slice(skip_grad_h, head_count, head_start, 0)
    in_grad = contract(hidden, proj_grad, 0, 0)
    step_w_grad = contract(hidden, step_back, 0, 0)
    hidden_grad = contract(proj_grad, w_in, 1, 1) + contract(step_back, w_step, 1, 1)
    resid_grad, norm_gain_grad = rms_backward(residual, norm_f, scale_in, hidden_grad)
    input_grad = out_cotangent.astype(jnp.float32) + resid_grad
    fsdp_count = lax.axis_size("fsdp")
    seq_total = lax.axis_size("seq")

    def spread_heads(gradient):
        return jnp.tile(gradient.reshape(fsdp_count, -1), (seq_total, 1)).reshape(-1)

    blocks = (
        lax.psum_scatter(
            reorder(in_grad, 0, fsdp_count, seq_total),
            ("seq", "fsdp"),
            scatter_dimension=0,
            tiled=True,
        ),
        lax.psum_scatter(
            reorder(step_w_grad, 0, fsdp_count, seq_total),
            ("seq", "fsdp"),
            scatter_dimension=0,
            tiled=True,
        ),
        lax.psum_scatter(
            reorder(kernel_grad, 1, fsdp_count, seq_total),
            ("seq", "fsdp"),
            scatter_dimension=1,
            tiled=True,
        ),
        lax.psum_scatter(
            reorder(bias_grad, 0, fsdp_count, seq_total),
            ("seq", "fsdp"),
            scatter_dimension=0,
            tiled=True,
        ),
        lax.psum_scatter(
            spread_heads(step_bias_grad), ("seq", "fsdp"), scatter_dimension=0, tiled=True
        ),
        lax.psum_scatter(
            spread_heads(decay_grad), ("seq", "fsdp"), scatter_dimension=0, tiled=True
        ),
        lax.psum_scatter(spread_heads(skip_grad), ("seq", "fsdp"), scatter_dimension=0, tiled=True),
        lax.psum_scatter(
            reorder(gate_gain_grad, 0, fsdp_count, seq_total),
            ("seq", "fsdp"),
            scatter_dimension=0,
            tiled=True,
        ),
        lax.psum_scatter(
            reorder(norm_gain_grad, 0, fsdp_count, seq_total),
            ("seq", "fsdp"),
            scatter_dimension=0,
            tiled=True,
        ),
        lax.psum_scatter(
            reorder(out_grad, 0, fsdp_count, seq_total),
            ("seq", "fsdp"),
            scatter_dimension=0,
            tiled=True,
        ),
    )
    joined = (
        lax.all_gather(blocks[0], "seq", axis=0, tiled=True),
        lax.all_gather(blocks[1], "seq", axis=0, tiled=True),
        lax.all_gather(blocks[2], "seq", axis=1, tiled=True),
        lax.all_gather(blocks[3], "seq", axis=0, tiled=True),
        lax.all_gather(blocks[7], "seq", axis=0, tiled=True),
        lax.all_gather(blocks[8], "seq", axis=0, tiled=True),
        lax.all_gather(blocks[9], "seq", axis=0, tiled=True),
    )
    totals = (
        joined[0],
        joined[1],
        joined[2],
        joined[3],
        blocks[4],
        blocks[5],
        blocks[6],
        joined[4],
        joined[5],
        joined[6],
    )
    return (
        block_out[None],
        input_grad[None],
        totals[0],
        totals[1],
        totals[2],
        totals[3],
        totals[4],
        totals[5],
        totals[6],
        totals[7],
        totals[8],
        totals[9],
    )


def solution(mesh):
    placed = (
        P("fsdp", "seq", None),
        P("fsdp", None),
        P("fsdp", None),
        P(None, "fsdp"),
        P("fsdp"),
        P("fsdp"),
        P("fsdp"),
        P("fsdp"),
        P("fsdp"),
        P("fsdp"),
        P("fsdp", None),
        P("fsdp", "seq", None),
    )
    return jax.shard_map(
        shards,
        mesh=mesh,
        in_specs=placed,
        out_specs=(
            P("fsdp", "seq", None),
            P("fsdp", "seq", None),
            P("fsdp", None),
            P("fsdp", None),
            P(None, "fsdp"),
            P("fsdp"),
            P("fsdp"),
            P("fsdp"),
            P("fsdp"),
            P("fsdp"),
            P("fsdp"),
            P("fsdp", None),
        ),
        check_vma=False,
    )
```

profile of v0, /device:TPU:0, one launch (start us, length us, event | category | flops | bytes accessed | tf_op | source)
XLA Modules:
  0.0 1683.6 jit_solution(14580512450812876870)
XLA Ops:
  28.3 108.3 %all-gather.9.cloned.1.call-done = bf16[1536,6400]{1,0:T(8,128)(2,1)} async-done(((bf16[384,6400]{1,0:T(8,128)(2,1)}), bf16[1536,6400]{1,0:T(8,128)(2,1)}) %all-gather.9.cloned.1.call-update) | async-done | bytes 19660816 | tf_op jit(solution)/shard_map/all_gather | solution.py:126
  136.7 9.4 convolution_convert_fusion
  154.5 12.8 all-to-all-done.2
  211.3 74.2 %while.41 = (s32[]{:T(128)}, f32[6,64,128]{2,1,0:T(8,128)S(1)}, f32[4,256,6,64]{1,0,3,2:T(4,128)}, f32[4,6,64,128]{3,2,1,0:T(8,128)}, f32[4,256,6]{1,2,0:T(8,128...) while((s32[]{:T(128)}, f32[6,64,128]{2,1,0:T(8,128)S(1)}, ...), condition=%wide.region_4.5_spmd.clone, body=%wide.region_1.4_spmd.clone.sunk | while | flops 706957824 | bytes 5773208 | solution.py:45
  220.3 9.5 dynamic_update_slice.89
  238.8 9.5 dynamic_update_slice.89
  257.4 9.5 dynamic_update_slice.89
  275.9 9.5 dynamic_update_slice.89
  310.4 14.1 all-to-all-done.4
  346.8 14.6 all-to-all-done.5
  376.5 167.4 %while.42 = (s32[]{:T(128)}, f32[6]{0:T(128)}, f32[6,64,128]{2,1,0:T(8,128)S(1)}, f32[4,256,6,64]{1,0,3,2:T(4,128)}, f32[4,256,6]{1,2,0:T(8,128)}, /*index=5*/f3...) while((s32[]{:T(128)}, f32[6]{0:T(128)}, ...), condition=%wide.region_20.21_spmd.clone, body=%wide.region_7.20_spmd.clone.sunk | while | flops 1669247488 | bytes 18030544 | solution.py:45
  390.1 7.6 reduce-window.74
  402.7 9.5 dynamic_update_slice.93
  444.6 9.5 dynamic_update_slice.93
  486.4 9.5 dynamic_update_slice.93
  528.3 9.5 dynamic_update_slice.93
  575.7 9.9 all_to_all.141
  595.2 13.1 all-to-all-done.6
  613.6 21.0 %all-to-all-done.7 = bf16[8,128,384]{2,1,0:T(8,128)(2,1)} async-done(((bf16[8,128,384]{2,1,0:T(8,128)(2,1)}), bf16[8,128,384]{2,1,0:T(8,128)(2,1)}, u32[]{:S(2)}, u32[]{:S(2)}) %all-to-all-start.7) | async-done | bytes 786464 | tf_op jit(solution)/shard_map/all_to_all | solution.py:233
  639.3 12.3 fusion.152
  653.8 20.1 %convolution_bitcast_fusion.2 = f32[8,4,48,6400]{3,2,0,1:T(8,128)} fusion(bf16[4,8,48,128]{3,2,1,0:T(8,128)(2,1)S(1)} %bitcast.577, bf16[128,6400]{1,0:T(8,128)(2,1)} %constant_dynamic-update-slice_fusion), kind=kOutput, calls=%fused_computation.128 | convolution fusion | flops 2516582400 | bytes 41353216 | tf_op jit(solution)/shard_map/dot_general | solution.py:93
  673.9 28.6 %copy.323 = f32[8,4,48,6400]{3,2,1,0:T(8,128)} copy(f32[8,4,48,6400]{3,2,0,1:T(8,128)} %convolution_bitcast_fusion.2) | data formatting | bytes 78643200 | tf_op jit(solution)/shard_map/transpose | solution.py:101
  711.7 130.3 %reduce-scatter.12.cloned.1.call-done = f32[96,1536]{1,0:T(8,128)} async-done(((f32[3072,1536]{1,0:T(8,128)}), f32[96,1536]{1,0:T(8,128)}) %reduce-scatter.12.cloned.1.call-update) | async-done | bytes 589840 | tf_op jit(solution)/shard_map/reduce_scatter | solution.py:317
  842.1 364.2 %reduce-scatter.10.cloned.1.call-done = f32[48,6400]{1,0:T(8,128)} async-done(((f32[1536,6400]{1,0:T(8,128)}), f32[48,6400]{1,0:T(8,128)}) %reduce-scatter.10.cloned.1.call-update) | async-done | bytes 1228816 | tf_op jit(solution)/shard_map/reduce_scatter | solution.py:274
  1214.8 123.9 %all-reduce.33.cloned.1.call-done = (f32[4,3328]{1,0:T(4,128)}, f32[3328]{0:T(1024)}, f32[384]{0:T(512)}, f32[384]{0:T(512)}, f32[384]{0:T(512)}, /*index=5*/f32[3072]{0:T(1024)}, f32[1536]{0:T(1024)}) async-done(((f32[4,3328]{1,0:T(4,128)}, f32[3328]{0:T(1024)}, f32[384]{0:T(512)}, f32[384]{0:T(512)}, f32[384]{0:T(512)}, /*index=5*/f32[3072]{0:T(1024)}, f32[1536]{0:T(1024)}), (f32[4,3328]{1,0:T(4,128)}, ...) | async-done | bytes 89616
  1339.5 27.0 %all-gather.3 = f32[8,104,4]{1,2,0:T(4,128)S(1)} all-gather(f32[1,104,4]{1,2,0:T(4,128)S(1)} %dynamic-slice_bitcast_fusion.7), channel_id=1, replica_groups=mesh['seq'=8,'fsdp'=4] {'seq'}, dimensions={0}, use_global_device_ids=true | all-gather | bytes 14976 | tf_op jit(solution)/shard_map/all_gather | solution.py:327
  1373.5 35.5 %all-reduce.29 = (f32[832]{0:T(1024)}, f32[768]{0:T(1024)}, f32[384]{0:T(512)}) all-reduce(f32[832]{0:T(1024)S(1)} %dynamic-slice_dynamic-update-slice_fusion.2, f32[768]{0:T(1024)S(1)} %dynamic-slice_dynamic-update-slice_fusion.1, f32[384]{0:T(512)S(1)} %dynamic-slice_dynamic-update-slice_fusion), channel_id=1, replica_groups=mesh['seq'=8,'fsdp'=4] {'seq'}, use_global_device_ids=true, to_apply=%add.18 | all-reduce | flops 1984 | bytes 15872
  1409.1 32.7 %reduce-scatter.14.cloned.1.call-done = f32[48,48]{1,0:T(8,128)} async-done(((f32[1536,48]{1,0:T(8,128)}), f32[48,48]{1,0:T(8,128)}) %reduce-scatter.14.cloned.1.call-update) | async-done | bytes 9232 | tf_op jit(solution)/shard_map/reduce_scatter | solution.py:280
  1441.8 32.1 %all_gather.62 = f32[384,48]{1,0:T(8,128)S(1)} all-gather(f32[48,48]{1,0:T(8,128)} %reduce-scatter.14.cloned.1.call-done), channel_id=1, replica_groups=mesh['seq'=8,'fsdp'=4] {'seq'}, dimensions={0}, use_global_device_ids=true | all-gather | bytes 82944 | tf_op jit(solution)/shard_map/all_gather | solution.py:326
  1474.6 48.8 %all-gather.15.cloned.1.call-done = f32[768,1536]{1,0:T(8,128)} async-done(((f32[96,1536]{1,0:T(8,128)}), f32[768,1536]{1,0:T(8,128)}) %all-gather.15.cloned.1.call-update) | async-done | bytes 4718608 | tf_op jit(solution)/shard_map/all_gather | solution.py:331
  1523.4 142.8 %all-gather.13.cloned.1.call-done = f32[384,6400]{1,0:T(8,128)} async-done(((f32[48,6400]{1,0:T(8,128)}), f32[384,6400]{1,0:T(8,128)}) %all-gather.13.cloned.1.call-update) | async-done | bytes 9830416 | tf_op jit(solution)/shard_map/all_gather | solution.py:325
  1666.2 8.4 copy.536
  (648 shorter events, 369.9 us)
Async XLA Ops:
  7.2 129.5 %all-gather.9.cloned.1.call-start = ((), (), s32[]{:S(2)}) async-start(), calls=%async_computation.13 | async-start | bytes 24576000 | tf_op jit(solution)/shard_map/all_gather | solution.py:126
  14.2 122.5 %copy-start.41 = (f32[1536]{0:T(1024)}, f32[1536]{0:T(1024)S(1)}, u32[]{:S(2)}) copy-start(f32[1536]{0:T(1024)S(1)} %reshape.548) | copy-start | bytes 18436
  20.7 116.0 %copy-start.58 = (f32[128]{0:T(128)}, f32[128]{0:T(128)S(1)}, u32[]{:S(2)}) copy-start(f32[128]{0:T(128)S(1)} %get-tuple-element.798) | copy-start | bytes 1540
  21.6 124.5 %all-to-all-start = ((bf16[128,8,6]{0,2,1:T(8,128)(2,1)}), bf16[128,8,6]{0,2,1:T(8,128)(2,1)S(1)}, u32[]{:S(2)}, u32[]{:S(2)}) async-start(bf16[128,8,6]{0,2,1:T(8,128)(2,1)} %all_to_all.106), calls=%async_computation | async-start | bytes 32768 | tf_op jit(solution)/shard_map/all_to_all | solution.py:173
  27.6 297.5 %all-gather.11.cloned.1.call-start = ((), (), s32[]{:S(2)}) async-start(), calls=%async_computation.14 | async-start | bytes 11796480 | tf_op jit(solution)/shard_map/all_gather | solution.py:135
  146.1 41.3 %copy-start.43 = (bf16[128,8,6]{0,2,1:T(8,128)(2,1)}, bf16[128,8,6]{0,2,1:T(8,128)(2,1)S(1)}, u32[]{:S(2)}) copy-start(bf16[128,8,6]{0,2,1:T(8,128)(2,1)S(1)} %all-to-all-done) | copy-start | bytes 36868
  146.9 20.4 %all-to-all-start.2 = ((bf16[128,8,256]{2,0,1:T(8,128)(2,1)}), bf16[128,8,256]{2,0,1:T(8,128)(2,1)S(1)}, u32[]{:S(2)}, u32[]{:S(2)}) async-start(bf16[128,8,256]{2,0,1:T(8,128)(2,1)} %tile.28), calls=%async_computation.2 | async-start | bytes 1048576 | tf_op jit(solution)/shard_map/all_to_all | solution.py:174
  153.5 19.9 %copy-start.73 = (bf16[12]{0:T(256)(128)(2,1)S(1)}, bf16[12]{0:T(256)(128)(2,1)}, u32[]{:S(2)}) copy-start(bf16[12]{0:T(256)(128)(2,1)} %param.22) | copy-start | bytes 76
  153.5 20.1 %copy-start.65 = (bf16[832]{0:T(1024)(128)(2,1)S(1)}, bf16[832]{0:T(1024)(128)(2,1)}, u32[]{:S(2)}) copy-start(bf16[832]{0:T(1024)(128)(2,1)} %param.20) | copy-start | bytes 4996
  153.5 27.6 %copy-start.62 = (bf16[4,832]{1,0:T(4,128)(2,1)S(1)}, bf16[4,832]{1,0:T(4,128)(2,1)}, u32[]{:S(2)}) copy-start(bf16[4,832]{1,0:T(4,128)(2,1)} %param.19) | copy-start | bytes 19972
  153.6 34.0 %copy-start.28 = (bf16[128,3072]{1,0:T(8,128)(2,1)S(1)}, bf16[128,3072]{1,0:T(8,128)(2,1)}, u32[]{:S(2)}) copy-start(bf16[128,3072]{1,0:T(8,128)(2,1)} %get-tuple-element.791) | copy-start | bytes 2359300
  167.4 28.8 %copy-start.23 = (bf16[128,8,256]{2,0,1:T(8,128)(2,1)}, bf16[128,8,256]{2,0,1:T(8,128)(2,1)S(1)}, u32[]{:S(2)}) copy-start(bf16[128,8,256]{2,0,1:T(8,128)(2,1)S(1)} %all-to-all-done.2) | copy-start | bytes 1572868
  167.4 24.0 %all-to-all-start.1 = ((bf16[128,8,384]{2,0,1:T(8,128)(2,1)}), bf16[128,8,384]{2,0,1:T(8,128)(2,1)S(1)}, u32[]{:S(2)}, u32[]{:S(2)}) async-start(bf16[128,8,384]{2,0,1:T(8,128)(2,1)} %bitcast.418), calls=%async_computation.1 | async-start | bytes 1572864 | tf_op jit(solution)/shard_map/all_to_all | solution.py:166
  181.1 160.6 %copy-start.68 = (f32[48]{0:T(128)}, f32[48]{0:T(128)S(1)}, u32[]{:S(2)}) copy-start(f32[48]{0:T(128)S(1)} %convert_element_type.138) | copy-start | bytes 580
  187.1 108.4 %copy-start.55 = (f32[384]{0:T(512)}, f32[384]{0:T(512)S(1)}, u32[]{:S(2)}) copy-start(f32[384]{0:T(512)S(1)} %mul.640) | copy-start | bytes 4612
  191.4 99.3 %all-to-all-start.3 = ((bf16[128,8,384]{0,2,1:T(8,128)(2,1)}), bf16[128,8,384]{0,2,1:T(8,128)(2,1)}, u32[]{:S(2)}, u32[]{:S(2)}) async-start(bf16[128,8,384]{0,2,1:T(8,128)(2,1)} %bitcast.18), calls=%async_computation.3 | async-start | bytes 1572864 | tf_op jit(solution)/shard_map/all_to_all | solution.py:165
  298.9 25.6 %all-to-all-start.4 = ((bf16[8,128,384]{2,1,0:T(8,128)(2,1)}), bf16[8,128,384]{2,1,0:T(8,128)(2,1)S(1)}, u32[]{:S(2)}, u32[]{:S(2)}) async-start(bf16[8,128,384]{2,1,0:T(8,128)(2,1)} %bitcast.580), calls=%async_computation.4 | async-start | bytes 1572864 | tf_op jit(solution)/shard_map/all_to_all | solution.py:206
  310.4 22.7 %copy-start.35 = (f32[4,1,768]{2,1,0:T(1,128)}, f32[4,1,768]{2,1,0:T(1,128)S(1)}, u32[]{:S(2)}) copy-start(f32[4,1,768]{2,1,0:T(1,128)S(1)} %convert_element_type.182) | copy-start | bytes 36868
  337.4 24.1 %all-to-all-start.5 = ((bf16[128,8,384]{0,2,1:T(8,128)(2,1)}), bf16[128,8,384]{0,2,1:T(8,128)(2,1)}, u32[]{:S(2)}, u32[]{:S(2)}) async-start(bf16[128,8,384]{0,2,1:T(8,128)(2,1)} %bitcast.583), calls=%async_computation.5 | async-start | bytes 1572864 | tf_op jit(solution)/shard_map/all_to_all | solution.py:219
  341.6 296.2 %reduce-scatter.8.cloned.1.call-start = ((), (), s32[]{:S(2)}) async-start(), calls=%async_computation.15 | async-start | bytes 589824 | tf_op jit(solution)/shard_map/reduce_scatter | solution.py:244
  563.5 278.5 %reduce-scatter.12.cloned.1.call-start = ((), (), s32[]{:S(2)}) async-start(), calls=%async_computation.18 | async-start | bytes 19464192 | tf_op jit(solution)/shard_map/reduce_scatter | solution.py:317
  585.6 22.7 %all-to-all-start.6 = ((bf16[8,128,384]{2,1,0:T(8,128)(2,1)}), bf16[8,128,384]{2,1,0:T(8,128)(2,1)S(1)}, u32[]{:S(2)}, u32[]{:S(2)}) async-start(bf16[8,128,384]{2,1,0:T(8,128)(2,1)} %bitcast.29), calls=%async_computation.6 | async-start | bytes 1572864 | tf_op jit(solution)/shard_map/all_to_all | solution.py:230
  608.3 26.4 %all-to-all-start.7 = ((bf16[8,128,384]{2,1,0:T(8,128)(2,1)}), bf16[8,128,384]{2,1,0:T(8,128)(2,1)}, u32[]{:S(2)}, u32[]{:S(2)}) async-start(bf16[8,128,384]{2,1,0:T(8,128)(2,1)} %bitcast.584), calls=%async_computation.7 | async-start | bytes 1572864 | tf_op jit(solution)/shard_map/all_to_all | solution.py:233
  612.5 593.8 %reduce-scatter.10.cloned.1.call-start = ((), (), s32[]{:S(2)}) async-start(), calls=%async_computation.16 | async-start | bytes 40550400 | tf_op jit(solution)/shard_map/reduce_scatter | solution.py:274
  613.6 22.3 %copy-start.27 = (bf16[8,16,8,384]{3,2,0,1:T(8,128)(2,1)S(1)}, bf16[8,16,8,384]{3,2,0,1:T(8,128)(2,1)}, u32[]{:S(2)}) copy-start(bf16[8,16,8,384]{3,2,0,1:T(8,128)(2,1)} %copy.389) | copy-start | bytes 2359300
  702.5 636.2 %all-reduce.33.cloned.1.call-start = ((), (), s32[]{:S(2)}) async-start(), calls=%async_computation.21 | async-start | bytes 192512
  710.4 731.4 %reduce-scatter.14.cloned.1.call-start = ((), (), s32[]{:S(2)}) async-start(), calls=%async_computation.20 | async-start | bytes 811008 | tf_op jit(solution)/shard_map/reduce_scatter | solution.py:280
  711.6 494.7 %copy-start.74 = (u32[32]{0:T(128)S(1)}, u32[32]{0:T(128)}, u32[]{:S(2)}) copy-start(u32[32]{0:T(128)} %constant.200) | copy-start | bytes 388
  711.6 497.3 %copy-start.36 = (f32[4,1,768]{2,1,0:T(1,128)S(1)}, f32[4,1,768]{2,1,0:T(1,128)}, u32[]{:S(2)}) copy-start(f32[4,1,768]{2,1,0:T(1,128)} %copy-done.35) | copy-start | bytes 36868
  711.6 497.3 %copy-start.61 = (f32[128]{0:T(128)S(1)}, f32[128]{0:T(128)}, u32[]{:S(2)}) copy-start(f32[128]{0:T(128)} %copy-done.60) | copy-start | bytes 1540
  711.7 811.7 %all-gather.15.cloned.1.call-start = ((), (), s32[]{:S(2)}) async-start(), calls=%async_computation.19 | async-start | bytes 5308416 | tf_op jit(solution)/shard_map/all_gather | solution.py:331
  842.1 824.1 %all-gather.13.cloned.1.call-start = ((), (), s32[]{:S(2)}) async-start(), calls=%async_computation.17 | async-start | bytes 11059200 | tf_op jit(solution)/shard_map/all_gather | solution.py:325
  (79 other events, 459.6 us)
Sparse Core Ops, SparseCore 0:
  9.6 127.0 all-gather.8
  138.2 64.7 all-gather.10
  563.6 63.3 reduce-scatter.7
  633.3 208.7 reduce-scatter.11
  848.3 357.9 reduce-scatter.9
  1213.8 124.8 all-reduce.32
  1344.4 97.3 reduce-scatter.13
  1444.0 79.3 all-gather.14
  1525.6 140.5 all-gather.12
where the time goes:
time: 1690 us; the launch traced here: 1680 us
  waiting for transfers between devices  1030 us (61%)
  local copies, waits for them, and re-layouts  232 us (14%)
  blocking collectives  135 us (8%)
  matrix products  132 us (8%)
  other arithmetic  96 us (6%)
  starting transfers between devices  38.3 us (2%)
  between operations  18.4 us (1%)
    reduce_scatter x1, waiting for transfers between devices, shards(): lax.psum_scatter(reorder(in_grad, 0, fsdp_count, seq_total), ('seq', 'fsd...  364 us
    all_gather x1, waiting for transfers between devices, shards(): lax.all_gather(blocks[0], 'seq', axis=0, tiled=True)  143 us
    reduce_scatter x1, waiting for transfers between devices, shards(): lax.psum_scatter(reorder(out_grad, 0, fsdp_count, seq_total), ('seq', 'fs...  130 us
    unnamed x10, waiting for transfers between devices  125 us
    all_gather x1, waiting for transfers between devices, shards(): lax.all_gather(in_weight, 'fsdp', axis=0, tiled=True)  108 us
    dynamic_update_slice x16, local copies, waits for them, and re-layouts, ssd_scan(): finals, outputs = lax.scan(jax.checkpoint(advance), carried, pieces)  79.5 us
    another operation x33, other arithmetic  50.7 us
    all_gather x1, waiting for transfers between devices, shards(): lax.all_gather(blocks[9], 'seq', axis=0, tiled=True)  48.8 us
  transfers between devices with their start and end apart: 17, of which 13 were waited for; matrix products, arithmetic and copies ran while one was open for 14% of the time, Pallas kernels for 0%

commit v1 on v0

--- a/solution.py
+++ b/solution.py
@@ -1,3 +1,4 @@
+import functools
 import jax
 import jax.numpy as jnp
 from jax import lax
@@ -7,6 +8,36 @@
 BLOCK = 256
 epsilon = 1e-05
 highest = lax.Precision.HIGHEST
+
+
+def _play_seats_all(frame_in, d_out):
+    frame_in = jnp.moveaxis(frame_in, 0, d_out)
+    tile_out = frame_in.shape
+    res = frame_in.reshape(
+        *tile_out[:d_out], tile_out[d_out] * tile_out[d_out + 1], *tile_out[d_out + 2 :]
+    )
+    return res
+
+
+def reach_rates(in_array, a_name):
+    current_block, long_array = (lax.axis_size(a_name), lax.axis_index(a_name))
+    a_next, met_up = (in_array[None], 1)
+    while met_up < current_block:
+        tall = lax.ppermute(
+            a_next, axis_name=a_name, perm=[(u, u ^ met_up) for u in range(current_block)]
+        )
+        r1 = long_array & met_up == 0
+        a_next = jnp.concatenate([jnp.where(r1, a_next, tall), jnp.where(r1, tall, a_next)])
+        met_up *= 2
+    return a_next
+
+
+def vector_check(field, xin, ndim_at):
+    d_next = _play_seats_all(reach_rates(field, xin), ndim_at)
+    return d_next
+
+
+check_trees = functools.partial(vector_check, xin="fsdp", ndim_at=0)
 
 
 def block_step(carried, pieces, decay_rate):
@@ -123,7 +154,7 @@
     cotangent,
 ):
     gathered = (
-        lax.all_gather(in_weight, "fsdp", axis=0, tiled=True),
+        check_trees(in_weight),
         lax.all_gather(step_weight, "fsdp", axis=0, tiled=True),
         lax.all_gather(conv_kernel, "fsdp", axis=1, tiled=True),
         lax.all_gather(conv_bias, "fsdp", axis=0, tiled=True),

time: 1690 us -> 1910 us (1.13)
  blocking collectives: 135 us -> 391 us
  waiting for transfers between devices: 1030 us -> 929 us
  other arithmetic: 96 us -> 140 us
    all_gather x1, blocking collectives: 6.18 us -> 263 us  [shards(): lax.all_gather(norm_gain, 'fsdp', axis=0, tiled=True)]
    all_gather x1 -> x0, waiting for transfers between devices: 108 us -> none  [shards(): lax.all_gather(in_weight, 'fsdp', axis=0, tiled=True)]
    select_n x0 -> x2, other arithmetic: none -> 19.9 us  [reach_rates(): jnp.where(r1, a_next, tall)]
    unnamed x173 -> x171, local copies, waits for them, and re-layouts: 41.2 us -> 42.9 us
    unnamed x10 -> x9, waiting for transfers between devices: 125 us -> 124 us
  transfers between devices with their start and end apart: 17 -> 18, of which waited for: 13 -> 13; matrix products, arithmetic and copies ran while one was open for 14% -> 14% of each run, Pallas kernels for 0% -> 0%
where the time goes in v1:
time: 1910 us; the launch traced here: 1900 us
  waiting for transfers between devices  929 us (49%)
  blocking collectives  391 us (20%)
  local copies, waits for them, and re-layouts  239 us (13%)
  other arithmetic  140 us (7%)
  matrix products  135 us (7%)
  starting transfers between devices  41.2 us (2%)
    reduce_scatter x1, waiting for transfers between devices, shards(): lax.psum_scatter(reorder(in_grad, 0, fsdp_count, seq_total), ('seq', 'fsd...  364 us
    all_gather x1, blocking collectives, shards(): lax.all_gather(norm_gain, 'fsdp', axis=0, tiled=True)  263 us
    all_gather x1, waiting for transfers between devices, shards(): lax.all_gather(blocks[0], 'seq', axis=0, tiled=True)  143 us
    reduce_scatter x1, waiting for transfers between devices, shards(): lax.psum_scatter(reorder(out_grad, 0, fsdp_count, seq_total), ('seq', 'fs...  131 us
    unnamed x9, waiting for transfers between devices  124 us
    dynamic_update_slice x16, local copies, waits for them, and re-layouts, ssd_scan(): finals, outputs = lax.scan(jax.checkpoint(advance), carried, pieces)  79.4 us
    another operation x33, other arithmetic  53.5 us
    all_gather x1, waiting for transfers between devices, shards(): lax.all_gather(blocks[9], 'seq', axis=0, tiled=True)  48.8 us
  transfers between devices with their start and end apart: 18, of which 13 were waited for; matrix products, arithmetic and copies ran while one was open for 14% of the time, Pallas kernels for 0%

profile of v1, /device:TPU:0, one launch (start us, length us, event | category | flops | bytes accessed | tf_op | source)
XLA Modules:
  0.0 1895.1 jit_solution(5513493673933471757)
XLA Ops:
  24.2 8.6 pad_maximum_fusion.1
  35.8 263.3 %all-gather = bf16[4,1,384]{2,1,0:T(2,128)(2,1)S(1)} all-gather(bf16[1,1,384]{2,1,0:T(2,128)(2,1)S(1)} %reshape.558), channel_id=1, replica_groups=mesh['seq'=8,'fsdp'=4] {'fsdp'}, dimensions={0}, use_global_device_ids=true | all-gather | bytes 3840 | tf_op jit(solution)/shard_map/all_gather | solution.py:165
  312.4 11.6 broadcast_select_fusion.3
  346.2 13.3 all-to-all-done.2
  403.6 87.3 %while.41 = (s32[]{:T(128)}, f32[6,64,128]{2,1,0:T(8,128)S(1)}, f32[4,256,6,64]{1,0,3,2:T(4,128)}, f32[4,6,64,128]{3,2,1,0:T(8,128)}, f32[4,256,6]{1,2,0:T(8,128...) while((s32[]{:T(128)}, f32[6,64,128]{2,1,0:T(8,128)S(1)}, ...), condition=%wide.region_4.5_spmd.clone, body=%wide.region_1.4_spmd.clone.sunk | while | flops 706957824 | bytes 5768624 | solution.py:76
  415.9 9.5 dynamic_update_slice.89
  437.7 9.5 dynamic_update_slice.89
  459.5 9.5 dynamic_update_slice.89
  481.4 9.5 dynamic_update_slice.89
  517.2 13.7 all-to-all-done.4
  553.2 14.6 all-to-all-done.5
  582.8 171.7 %while.42 = (s32[]{:T(128)}, f32[6]{0:T(128)}, f32[6,64,128]{2,1,0:T(8,128)}, f32[4,256,6,64]{1,0,3,2:T(4,128)}, f32[4,256,6]{1,2,0:T(8,128)}, /*index=5*/f32[4,...) while((s32[]{:T(128)}, f32[6]{0:T(128)}, ...), condition=%wide.region_20.21_spmd.clone, body=%wide.region_7.20_spmd.clone.sunk | while | flops 1669247488 | bytes 17047420 | solution.py:76
  609.5 9.5 dynamic_update_slice.93
  652.8 9.5 dynamic_update_slice.93
  696.0 9.5 dynamic_update_slice.93
  739.3 9.5 dynamic_update_slice.93
  786.4 10.0 all_to_all.141
  805.9 13.2 all-to-all-done.6
  825.0 20.2 %all-to-all-done.7 = bf16[8,128,384]{2,1,0:T(8,128)(2,1)S(1)} async-done(((bf16[8,128,384]{2,1,0:T(8,128)(2,1)}), bf16[8,128,384]{2,1,0:T(8,128)(2,1)S(1)}, u32[]{:S(2)}, u32[]{:S(2)}) %all-to-all-start.7) | async-done | bytes 786464 | tf_op jit(solution)/shard_map/all_to_all | solution.py:264
  847.4 13.8 fusion.121
  864.7 19.5 %convolution_bitcast_fusion.2 = f32[8,4,48,6400]{3,2,0,1:T(8,128)} fusion(bf16[4,8,48,128]{3,2,1,0:T(8,128)(2,1)} %bitcast.610, bf16[128,6400]{1,0:T(8,128)(2,1)S(1)} %constant_dynamic-update-slice_fusion), kind=kOutput, calls=%fused_computation.129 | convolution fusion | flops 2516582400 | bytes 41353216 | tf_op jit(solution)/shard_map/dot_general | solution.py:124
  884.2 28.5 %copy.323 = f32[8,4,48,6400]{3,2,1,0:T(8,128)} copy(f32[8,4,48,6400]{3,2,0,1:T(8,128)} %convolution_bitcast_fusion.2) | data formatting | bytes 78643200 | tf_op jit(solution)/shard_map/transpose | solution.py:132
  922.0 131.4 %reduce-scatter.12.cloned.1.call-done = f32[96,1536]{1,0:T(8,128)} async-done(((f32[3072,1536]{1,0:T(8,128)}), f32[96,1536]{1,0:T(8,128)}) %reduce-scatter.12.cloned.1.call-update) | async-done | bytes 589840 | tf_op jit(solution)/shard_map/reduce_scatter | solution.py:348
  1053.5 364.0 %reduce-scatter.10.cloned.1.call-done = f32[48,6400]{1,0:T(8,128)} async-done(((f32[1536,6400]{1,0:T(8,128)}), f32[48,6400]{1,0:T(8,128)}) %reduce-scatter.10.cloned.1.call-update) | async-done | bytes 1228816 | tf_op jit(solution)/shard_map/reduce_scatter | solution.py:305
  1426.0 123.8 %all-reduce.33.cloned.1.call-done = (f32[4,3328]{1,0:T(4,128)}, f32[3328]{0:T(1024)}, f32[384]{0:T(512)}, f32[384]{0:T(512)}, f32[384]{0:T(512)}, /*index=5*/f32[3072]{0:T(1024)}, f32[1536]{0:T(1024)}) async-done(((f32[4,3328]{1,0:T(4,128)}, f32[3328]{0:T(1024)}, f32[384]{0:T(512)}, f32[384]{0:T(512)}, f32[384]{0:T(512)}, /*index=5*/f32[3072]{0:T(1024)}, f32[1536]{0:T(1024)}), (f32[4,3328]{1,0:T(4,128)}, ...) | async-done | bytes 89616
  1550.6 27.0 %all-gather.3 = f32[8,104,4]{1,2,0:T(4,128)S(1)} all-gather(f32[1,104,4]{1,2,0:T(4,128)S(1)} %dynamic-slice_bitcast_fusion.7), channel_id=1, replica_groups=mesh['seq'=8,'fsdp'=4] {'seq'}, dimensions={0}, use_global_device_ids=true | all-gather | bytes 14976 | tf_op jit(solution)/shard_map/all_gather | solution.py:358
  1584.6 35.6 %all-reduce.29 = (f32[832]{0:T(1024)}, f32[768]{0:T(1024)}, f32[384]{0:T(512)}) all-reduce(f32[832]{0:T(1024)S(1)} %dynamic-slice_dynamic-update-slice_fusion.2, f32[768]{0:T(1024)S(1)} %dynamic-slice_dynamic-update-slice_fusion.1, f32[384]{0:T(512)S(1)} %dynamic-slice_dynamic-update-slice_fusion), channel_id=1, replica_groups=mesh['seq'=8,'fsdp'=4] {'seq'}, use_global_device_ids=true, to_apply=%add.18 | all-reduce | flops 1984 | bytes 15872
  1620.2 32.6 %reduce-scatter.14.cloned.1.call-done = f32[48,48]{1,0:T(8,128)} async-done(((f32[1536,48]{1,0:T(8,128)}), f32[48,48]{1,0:T(8,128)}) %reduce-scatter.14.cloned.1.call-update) | async-done | bytes 9232 | tf_op jit(solution)/shard_map/reduce_scatter | solution.py:311
  1652.8 32.1 %all_gather.58 = f32[384,48]{1,0:T(8,128)S(1)} all-gather(f32[48,48]{1,0:T(8,128)} %reduce-scatter.14.cloned.1.call-done), channel_id=1, replica_groups=mesh['seq'=8,'fsdp'=4] {'seq'}, dimensions={0}, use_global_device_ids=true | all-gather | bytes 82944 | tf_op jit(solution)/shard_map/all_gather | solution.py:357
  1685.6 48.8 %all-gather.12.cloned.1.call-done = f32[768,1536]{1,0:T(8,128)} async-done(((f32[96,1536]{1,0:T(8,128)}), f32[768,1536]{1,0:T(8,128)}) %all-gather.12.cloned.1.call-update) | async-done | bytes 4718608 | tf_op jit(solution)/shard_map/all_gather | solution.py:362
  1734.4 142.8 %all-gather.10.cloned.1.call-done = f32[384,6400]{1,0:T(8,128)} async-done(((f32[48,6400]{1,0:T(8,128)}), f32[384,6400]{1,0:T(8,128)}) %all-gather.10.cloned.1.call-update) | async-done | bytes 9830416 | tf_op jit(solution)/shard_map/all_gather | solution.py:356
  1877.2 8.4 copy.536
  (627 shorter events, 422.0 us)
Async XLA Ops:
  7.2 524.3 %all-gather.8.cloned.1.call-start = ((), (), s32[]{:S(2)}) async-start(), calls=%async_computation.13 | async-start | bytes 11796480 | tf_op jit(solution)/shard_map/all_gather | solution.py:166
  7.2 8.7 collective-permute-start
  32.9 266.3 %copy-start.50 = (bf16[384,48]{0,1:T(8,128)(2,1)S(1)}, bf16[384,48]{0,1:T(8,128)(2,1)}, u32[]{:S(2)}) copy-start(bf16[384,48]{0,1:T(8,128)(2,1)} %param.18) | copy-start | bytes 110596
  32.9 271.8 %copy-start.11 = (bf16[1,128,1536]{2,1,0:T(8,128)(2,1)S(1)}, bf16[1,128,1536]{2,1,0:T(8,128)(2,1)}, u32[]{:S(2)}) copy-start(bf16[1,128,1536]{2,1,0:T(8,128)(2,1)} %param.16) | copy-start | bytes 1179652
  32.9 279.5 %collective-permute-start.1 = (bf16[2,384,6400]{2,1,0:T(8,128)(2,1)}, bf16[2,384,6400]{2,1,0:T(8,128)(2,1)}, u32[]{:S(2)}, u32[]{:S(2)}) collective-permute-start(bf16[2,384,6400]{2,1,0:T(8,128)(2,1)} %pad_maximum_fusion.1), channel_id=1, source_target_pairs={{0,2},{1,3},{2,0},{3,1},{4,6},{5,7},{6,4},{7,5},{8,10},{9,11},{10,... | collective-permute-start | bytes 29491208 | tf_op jit(solution)/shard_map/ppermute | solution.py:26
  299.2 32.3 %copy-start.37 = (f32[1536]{0:T(1024)}, f32[1536]{0:T(1024)S(1)}, u32[]{:S(2)}) copy-start(f32[1536]{0:T(1024)S(1)} %reshape.566) | copy-start | bytes 18436
  305.4 26.1 %copy-start.54 = (f32[128]{0:T(128)}, f32[128]{0:T(128)S(1)}, u32[]{:S(2)}) copy-start(f32[128]{0:T(128)S(1)} %get-tuple-element.802) | copy-start | bytes 1540
  306.4 31.8 %all-to-all-start = ((bf16[128,8,6]{0,2,1:T(8,128)(2,1)}), bf16[128,8,6]{0,2,1:T(8,128)(2,1)S(1)}, u32[]{:S(2)}, u32[]{:S(2)}) async-start(bf16[128,8,6]{0,2,1:T(8,128)(2,1)} %all_to_all.106), calls=%async_computation | async-start | bytes 32768 | tf_op jit(solution)/shard_map/all_to_all | solution.py:204
  338.2 40.9 %copy-start.39 = (bf16[128,8,6]{0,2,1:T(8,128)(2,1)}, bf16[128,8,6]{0,2,1:T(8,128)(2,1)S(1)}, u32[]{:S(2)}) copy-start(bf16[128,8,6]{0,2,1:T(8,128)(2,1)S(1)} %all-to-all-done) | copy-start | bytes 36868
  339.0 20.4 %all-to-all-start.2 = ((bf16[128,8,256]{2,0,1:T(8,128)(2,1)}), bf16[128,8,256]{2,0,1:T(8,128)(2,1)S(1)}, u32[]{:S(2)}, u32[]{:S(2)}) async-start(bf16[128,8,256]{2,0,1:T(8,128)(2,1)} %tile.28), calls=%async_computation.2 | async-start | bytes 1048576 | tf_op jit(solution)/shard_map/all_to_all | solution.py:205
  345.2 27.9 %copy-start.58 = (bf16[4,832]{1,0:T(4,128)(2,1)S(1)}, bf16[4,832]{1,0:T(4,128)(2,1)}, u32[]{:S(2)}) copy-start(bf16[4,832]{1,0:T(4,128)(2,1)} %param.19) | copy-start | bytes 19972
  359.5 28.5 %copy-start.20 = (bf16[128,8,256]{2,0,1:T(8,128)(2,1)}, bf16[128,8,256]{2,0,1:T(8,128)(2,1)S(1)}, u32[]{:S(2)}) copy-start(bf16[128,8,256]{2,0,1:T(8,128)(2,1)S(1)} %all-to-all-done.2) | copy-start | bytes 1572868
  359.5 24.0 %all-to-all-start.1 = ((bf16[128,8,384]{2,0,1:T(8,128)(2,1)}), bf16[128,8,384]{2,0,1:T(8,128)(2,1)S(1)}, u32[]{:S(2)}, u32[]{:S(2)}) async-start(bf16[128,8,384]{2,0,1:T(8,128)(2,1)} %bitcast.450), calls=%async_computation.1 | async-start | bytes 1572864 | tf_op jit(solution)/shard_map/all_to_all | solution.py:197
  373.1 175.0 %copy-start.64 = (f32[48]{0:T(128)}, f32[48]{0:T(128)S(1)}, u32[]{:S(2)}) copy-start(f32[48]{0:T(128)S(1)} %convert_element_type.146) | copy-start | bytes 580
  378.9 123.5 %copy-start.51 = (f32[384]{0:T(512)}, f32[384]{0:T(512)S(1)}, u32[]{:S(2)}) copy-start(f32[384]{0:T(512)S(1)} %mul.654) | copy-start | bytes 4612
  383.5 113.4 %all-to-all-start.3 = ((bf16[128,8,384]{0,2,1:T(8,128)(2,1)}), bf16[128,8,384]{0,2,1:T(8,128)(2,1)}, u32[]{:S(2)}, u32[]{:S(2)}) async-start(bf16[128,8,384]{0,2,1:T(8,128)(2,1)} %bitcast.20), calls=%async_computation.3 | async-start | bytes 1572864 | tf_op jit(solution)/shard_map/all_to_all | solution.py:196
  390.9 111.5 %copy-start.1 = (f32[1024,640]{1,0:T(8,128)}, f32[1024,640]{1,0:T(8,128)S(1)}, u32[]{:S(2)}) copy-start(f32[1024,640]{1,0:T(8,128)S(1)} %get-tuple-element.768) | copy-start | bytes 7864324
  505.6 25.3 %all-to-all-start.4 = ((bf16[8,128,384]{2,1,0:T(8,128)(2,1)}), bf16[8,128,384]{2,1,0:T(8,128)(2,1)S(1)}, u32[]{:S(2)}, u32[]{:S(2)}) async-start(bf16[8,128,384]{2,1,0:T(8,128)(2,1)} %bitcast.613), calls=%async_computation.4 | async-start | bytes 1572864 | tf_op jit(solution)/shard_map/all_to_all | solution.py:237
  543.8 24.0 %all-to-all-start.5 = ((bf16[128,8,384]{0,2,1:T(8,128)(2,1)}), bf16[128,8,384]{0,2,1:T(8,128)(2,1)}, u32[]{:S(2)}, u32[]{:S(2)}) async-start(bf16[128,8,384]{0,2,1:T(8,128)(2,1)} %bitcast.617), calls=%async_computation.5 | async-start | bytes 1572864 | tf_op jit(solution)/shard_map/all_to_all | solution.py:250
  548.0 298.5 %reduce-scatter.8.cloned.1.call-start = ((), (), s32[]{:S(2)}) async-start(), calls=%async_computation.14 | async-start | bytes 589824 | tf_op jit(solution)/shard_map/reduce_scatter | solution.py:275
  774.2 279.2 %reduce-scatter.12.cloned.1.call-start = ((), (), s32[]{:S(2)}) async-start(), calls=%async_computation.17 | async-start | bytes 19464192 | tf_op jit(solution)/shard_map/reduce_scatter | solution.py:348
  796.3 22.8 %all-to-all-start.6 = ((bf16[8,128,384]{2,1,0:T(8,128)(2,1)}), bf16[8,128,384]{2,1,0:T(8,128)(2,1)S(1)}, u32[]{:S(2)}, u32[]{:S(2)}) async-start(bf16[8,128,384]{2,1,0:T(8,128)(2,1)} %bitcast.31), calls=%async_computation.6 | async-start | bytes 1572864 | tf_op jit(solution)/shard_map/all_to_all | solution.py:261
  819.1 26.1 %all-to-all-start.7 = ((bf16[8,128,384]{2,1,0:T(8,128)(2,1)}), bf16[8,128,384]{2,1,0:T(8,128)(2,1)S(1)}, u32[]{:S(2)}, u32[]{:S(2)}) async-start(bf16[8,128,384]{2,1,0:T(8,128)(2,1)} %bitcast.35), calls=%async_computation.7 | async-start | bytes 1572864 | tf_op jit(solution)/shard_map/all_to_all | solution.py:264
  822.8 594.8 %reduce-scatter.10.cloned.1.call-start = ((), (), s32[]{:S(2)}) async-start(), calls=%async_computation.15 | async-start | bytes 40550400 | tf_op jit(solution)/shard_map/reduce_scatter | solution.py:305
  912.8 637.1 %all-reduce.33.cloned.1.call-start = ((), (), s32[]{:S(2)}) async-start(), calls=%async_computation.20 | async-start | bytes 192512
  920.7 732.1 %reduce-scatter.14.cloned.1.call-start = ((), (), s32[]{:S(2)}) async-start(), calls=%async_computation.19 | async-start | bytes 811008 | tf_op jit(solution)/shard_map/reduce_scatter | solution.py:311
  921.9 495.6 %copy-start.70 = (u32[32]{0:T(128)S(1)}, u32[32]{0:T(128)}, u32[]{:S(2)}) copy-start(u32[32]{0:T(128)} %constant.207) | copy-start | bytes 388
  921.9 498.2 %copy-start.13 = (bf16[1,128,1536]{2,1,0:T(8,128)(2,1)S(1)}, bf16[1,128,1536]{2,1,0:T(8,128)(2,1)}, u32[]{:S(2)}) copy-start(bf16[1,128,1536]{2,1,0:T(8,128)(2,1)} %param.16) | copy-start | bytes 1179652
  921.9 498.2 %copy-start.32 = (f32[4,1,768]{2,1,0:T(1,128)S(1)}, f32[4,1,768]{2,1,0:T(1,128)}, u32[]{:S(2)}) copy-start(f32[4,1,768]{2,1,0:T(1,128)} %copy-done.31) | copy-start | bytes 36868
  921.9 498.2 %copy-start.57 = (f32[128]{0:T(128)S(1)}, f32[128]{0:T(128)}, u32[]{:S(2)}) copy-start(f32[128]{0:T(128)} %copy-done.56) | copy-start | bytes 1540
  922.0 812.4 %all-gather.12.cloned.1.call-start = ((), (), s32[]{:S(2)}) async-start(), calls=%async_computation.18 | async-start | bytes 5308416 | tf_op jit(solution)/shard_map/all_gather | solution.py:362
  1053.5 823.7 %all-gather.10.cloned.1.call-start = ((), (), s32[]{:S(2)}) async-start(), calls=%async_computation.16 | async-start | bytes 11059200 | tf_op jit(solution)/shard_map/all_gather | solution.py:356
  (67 other events, 453.5 us)
Sparse Core Ops, SparseCore 0:
  35.9 115.1 all-gather.7
  774.3 68.4 reduce-scatter.7
  849.3 204.1 reduce-scatter.11
  1059.7 357.7 reduce-scatter.9
  1424.9 124.8 all-reduce.32
  1555.4 97.3 reduce-scatter.13
  1655.0 79.3 all-gather.11
  1736.6 140.5 all-gather.9
